TPU v7x, 128 devices: a whole 4x4x4 slice. The times are simulated.
128 devices in a mesh: section: 4 (over x), dp: 32 (over y, z, core).
Axes of the slice: x: 4, y: 4, z: 4, core: 2. Of those that a mesh axis runs over, the one named last changes fastest.
Arguments:
- clip_pool: bfloat16 [1024, 256, 512], P('dp'), may hold values from -8 to 8
- clip_index: int32 [8, 128], P(None, 'dp'), may hold values from 0 to 31, as said below
- batch_order: int32 [8], replicated, may hold values from 0 to 7, each once
- tap_weights: bfloat16 [4, 3, 512, 512], P('section'), may hold values from -0.15625 to 0.15625
- out_weights: bfloat16 [4, 512, 512], P('section'), may hold values from -0.25 to 0.25
- norm_gains: bfloat16 [4, 512], P('section'), may hold values from 0.099609375 to 1.8984375
- quant_weight: bfloat16 [512, 18], replicated, may hold values from -0.25 to 0.25
- quant_bias: float32 [18], replicated, may hold values from -3 to 3
- post_weight: bfloat16 [18, 512], replicated, may hold values from -1.5 to 1.5
Outputs:
- row_error: float32 [8, 128, 256], P('section', 'dp')
- entropy_loss: float32 [8], replicated
Inputs may be any that keep to these rules, and one draw needn't show every extreme that they name: `clip_index`: entries index the clips of the replica that holds the column; over all 8 micro-batches, the 4 columns of one replica name each of its 32 clips exactly once. `batch_order`: each micro-batch number 0 to 7 once.
All inputs are finite; a program needn't handle non-finite values.
Results may differ from a plain program's by a relative error of at most 0.0015.
Values may be sent and summed in bfloat16 or wider, within the bound.
A program may use at most 128 MiB of HBM per device.

v0:
```python
import functools
import jax
import jax.numpy as jnp
from jax import lax
from jax.sharding import Mesh
from jax.sharding import PartitionSpec as P

SPATIAL = 64
DP = ("dp_0", "dp_1", "dp_2")
SECTION_DP = ("section", "dp_0", "dp_1", "dp_2")
norm_eps = 1e-06
quant_section = 1


def over_axes(array, axes):
    return functools.reduce(lax.psum, axes, array)


def run_block(current, tap_set, out_weight, gain_row):
    clip_count, row_count, channels = current.shape
    widened = current.astype(jnp.float32)
    scale = lax.rsqrt(jnp.mean(widened * widened, axis=-1, keepdims=True) + norm_eps)
    normed = (widened * scale * gain_row.astype(jnp.float32)).astype(jnp.bfloat16)
    flat = normed.reshape(-1, channels)
    mixed = jnp.zeros((clip_count, row_count, channels), jnp.float32)
    for k in range(tap_set.shape[0]):
        product = jnp.dot(flat, tap_set[k], preferred_element_type=jnp.float32).reshape(
            clip_count, row_count, channels
        )
        moved = jnp.pad(product, ((0, 0), (k * SPATIAL, 0), (0, 0)))[:, :row_count]
        mixed = mixed + moved
    activated = jax.nn.silu(mixed).astype(jnp.bfloat16)
    update = jnp.dot(
        activated.reshape(-1, channels), out_weight, preferred_element_type=jnp.float32
    )
    return (widened + update.reshape(clip_count, row_count, channels)).astype(jnp.bfloat16)


def quantize(current, quant_weight, quant_bias, post_weight):
    channels = current.shape[-1]
    logits = (
        jnp.dot(current.reshape(-1, channels), quant_weight, preferred_element_type=jnp.float32)
        + quant_bias
    )
    bit_prob = jax.nn.sigmoid(4.0 * logits)
    codes = (2.0 * bit_prob - 1.0).astype(jnp.bfloat16)
    quantized = jnp.dot(codes, post_weight, preferred_element_type=jnp.float32).astype(jnp.bfloat16)
    bit_sums = jnp.sum(bit_prob, axis=0)
    entropy_sum = -jnp.sum(
        bit_prob * jax.nn.log_sigmoid(4.0 * logits)
        + (1.0 - bit_prob) * jax.nn.log_sigmoid(-4.0 * logits)
    )
    return (quantized.reshape(current.shape), bit_sums, entropy_sum)


def squared_error(decoded, source):
    differ = decoded.astype(jnp.float32) - source.astype(jnp.float32)
    return jnp.mean(differ * differ, axis=-1)


def final_entropy(bit_buffer, entropy_buffer, batch_order, rows_total):
    marginal = bit_buffer / rows_total
    sample_entropy = entropy_buffer / rows_total
    averaged = jnp.zeros_like(marginal)
    running = marginal[batch_order[0]]
    for t in range(batch_order.shape[0]):
        if t > 0:
            running = 0.5 * running + 0.5 * marginal[batch_order[t]]
        averaged = averaged.at[batch_order[t]].set(running)
    smoothed = 0.05 + 0.9 * averaged
    code_entropy = -jnp.sum(
        smoothed * jnp.log(smoothed) + (1.0 - smoothed) * jnp.log(1.0 - smoothed), axis=-1
    )
    return sample_entropy - code_entropy


def on_device(
    clip_pool,
    clip_index,
    batch_order,
    tap_weights,
    out_weights,
    norm_gains,
    quant_weight,
    quant_bias,
    post_weight,
):
    section_id = lax.axis_index("section")
    sections = lax.axis_size("section")
    batches = batch_order.shape[0]
    clip_count = clip_index.shape[1]
    row_count = clip_pool.shape[1]
    rows_total = float(clip_count * lax.axis_size(DP) * row_count)
    bit_buffer = jnp.zeros((batches, quant_weight.shape[1]), jnp.float32)
    entropy_buffer = jnp.zeros((batches,), jnp.float32)
    all_taps, all_out, all_gains = (
        lax.all_gather(tap_weights, "section", axis=0, tiled=True),
        lax.all_gather(out_weights, "section", axis=0, tiled=True),
        lax.all_gather(norm_gains, "section", axis=0, tiled=True),
    )
    per_section = batches // sections
    error_list = []
    for i in range(per_section):
        batch_slot = section_id * per_section + i
        source = jnp.take(clip_pool, clip_index[batch_slot], axis=0)
        current = source
        for s in range(sections):
            current = run_block(current, all_taps[s], all_out[s], all_gains[s])
            if s == quant_section:
                current, bit_sums, entropy_sum = quantize(
                    current, quant_weight, quant_bias, post_weight
                )
                bit_buffer = bit_buffer.at[batch_slot].add(bit_sums)
                entropy_buffer = entropy_buffer.at[batch_slot].add(entropy_sum)
        error_list.append(squared_error(current, source))
    bit_buffer, entropy_buffer = (
        over_axes(bit_buffer, SECTION_DP),
        over_axes(entropy_buffer, SECTION_DP),
    )
    error_out = jnp.stack(error_list)
    losses = final_entropy(bit_buffer, entropy_buffer, batch_order, rows_total)
    return (error_out, losses)


def solution(mesh):
    torus = Mesh(
        mesh.devices.reshape(mesh.shape["section"], 4, 4, 2), ("section", "dp_0", "dp_1", "dp_2")
    )
    return jax.shard_map(
        on_device,
        mesh=torus,
        in_specs=(
            P(DP, None, None),
            P(None, DP),
            P(),
            P("section", None, None, None),
            P("section", None, None),
            P("section", None),
            P(),
            P(),
            P(),
        ),
        out_specs=(P("section", DP, None), P()),
        check_vma=False,
    )
```

profile of v0, /device:TPU:1, one launch (start us, length us, event | category | flops | bytes accessed | tf_op | source)
XLA Modules:
  0.0 248.7 jit_solution(16837074438808056096)
XLA Ops:
  7.2 0.7 all-gather.4.cloned.1.call-update
  8.0 0.7 all-gather.6.cloned.1.call-update
  8.7 0.7 fusion.181
  20.1 4.7 %gather_fusion = bf16[4,256,512]{2,1,0:T(8,128)(2,1)S(1)} fusion(bf16[32,256,512]{2,1,0:T(8,128)(2,1)} %param.35, s32[1024]{0:T(1024)S(1)} %pad_clamp_fusion.1), kind=kCustom, calls=%fused_computation.clone | custom fusion | bytes 2097168 | tf_op jit(solution)/shard_map/jit(_take)/gather | solution.py:105
  24.8 4.8 %gather_fusion.1 = bf16[4,256,512]{2,1,0:T(8,128)(2,1)S(1)} fusion(bf16[32,256,512]{2,1,0:T(8,128)(2,1)} %param.35, s32[1024]{0:T(1024)S(1)} %pad_clamp_fusion), kind=kCustom, calls=%fused_computation.1.clone | custom fusion | bytes 2097168 | tf_op jit(solution)/shard_map/jit(_take)/gather | solution.py:105
  34.9 10.8 %all-gather = bf16[4,1,512]{2,1,0:T(2,128)(2,1)S(1)} all-gather(bf16[1,1,512]{2,1,0:T(2,128)(2,1)S(1)} %bitcast.176), channel_id=1, replica_groups=mesh['section'=4,'dp_0'=4,'dp_1'=4,'dp_2'=2] {'section'}, dimensions={0}, use_global_device_ids=true | all-gather | bytes 5120 | tf_op jit(solution)/shard_map/all_gather | solution.py:99
  45.7 0.8 and_reduce_fusion.4
  46.5 0.9 and_reduce_fusion
  48.2 30.2 %all-gather.4.cloned.1.call-done = bf16[4,3,512,512]{3,2,1,0:T(8,128)(2,1)} async-done(((bf16[1,3,512,512]{3,2,1,0:T(8,128)(2,1)}), bf16[4,3,512,512]{3,2,1,0:T(8,128)(2,1)}) %all-gather.4.cloned.1.call-update) | async-done | bytes 6291472 | tf_op jit(solution)/shard_map/all_gather | solution.py:97
  78.5 3.1 %fusion.60 = f32[4,256,512]{2,1,0:T(8,128)} fusion(f32[4,256]{1,0:T(4,128)S(1)} %add_rsqrt_fusion.3, f32[512]{0:T(512)S(1)} %bitcast.189, bf16[4,3,512,512]{3,2,1,0:T(8,128)(2,1)} %all-gather.4.cloned.1.call-done, bf16[4,256,512]{2,1,0:T(8,128)(2,1)S(1)} %gather_fusion.1, pred[4]{0:T(512)(128)(4,1)S(1)} %get-tuple-element.209), kind=kOutput, calls=%fused_computation.107 | convolution fusion | flops 539492352 | bytes 3676164 | tf_op jit(solution)/shard_map/dot_general | solution.py:27
  81.6 3.2 %fusion.58 = f32[4,256,512]{2,1,0:T(8,128)} fusion(f32[4,256]{1,0:T(4,128)S(1)} %add_rsqrt_fusion.3, f32[512]{0:T(512)S(1)} %bitcast.190, bf16[4,3,512,512]{3,2,1,0:T(8,128)(2,1)} %all-gather.4.cloned.1.call-done, bf16[4,256,512]{2,1,0:T(8,128)(2,1)S(1)} %gather_fusion.1, pred[4]{0:T(512)(128)(4,1)S(1)} %get-tuple-element.209), kind=kOutput, calls=%fused_computation.106 | convolution fusion | flops 539492352 | bytes 3676164 | tf_op jit(solution)/shard_map/dot_general | solution.py:27
  84.8 26.6 %all-gather.6.cloned.1.call-done = bf16[4,512,512]{2,1,0:T(8,128)(2,1)} async-done(((bf16[1,512,512]{2,1,0:T(8,128)(2,1)}), bf16[4,512,512]{2,1,0:T(8,128)(2,1)}) %all-gather.6.cloned.1.call-update) | async-done | bytes 2097168 | tf_op jit(solution)/shard_map/all_gather | solution.py:98
  111.4 4.6 %fusion.24 = (f32[4,256]{1,0:T(4,128)S(1)}, bf16[4,256,512]{2,1,0:T(8,128)(2,1)}) fusion(bf16[4,512,512]{2,1,0:T(8,128)(2,1)} %all-gather.6.cloned.1.call-done, f32[4,256,512]{2,1,0:T(8,128)} %fusion.58, f32[4,256,512]{2,1,0:T(8,128)} %fusion.60, f32[4,256]{1,0:T(4,128)S(1)} %add_rsqrt_fusion.3, f32[512]{0:T(512)S(1)} %bitcast.191, ...), kind=kOutput, calls=%fused_computation.62 | convolution fusion | flops 1083702272 | bytes 8399872 | tf_op jit(solution)/shard_map/dot_general | solution.py:33
  116.1 3.5 %fusion.54 = f32[4,256,512]{2,1,0:T(8,128)} fusion(bf16[4,256,512]{2,1,0:T(8,128)(2,1)} %get-tuple-element.194, f32[4,256]{1,0:T(4,128)S(1)} %add_rsqrt_fusion.2, f32[512]{0:T(512)S(1)} %bitcast.183, bf16[4,3,512,512]{3,2,1,0:T(8,128)(2,1)} %all-gather.4.cloned.1.call-done), kind=kOutput, calls=%fused_computation.105 | convolution fusion | flops 538968064 | bytes 3676160 | tf_op jit(solution)/shard_map/dot_general | solution.py:27
  119.6 3.2 %fusion.52 = f32[4,256,512]{2,1,0:T(8,128)} fusion(bf16[4,256,512]{2,1,0:T(8,128)(2,1)S(1)} %copy-done.16, f32[4,256]{1,0:T(4,128)S(1)} %add_rsqrt_fusion.2, f32[512]{0:T(512)S(1)} %bitcast.184, bf16[4,3,512,512]{3,2,1,0:T(8,128)(2,1)} %all-gather.4.cloned.1.call-done), kind=kOutput, calls=%fused_computation.104 | convolution fusion | flops 538968064 | bytes 3676160 | tf_op jit(solution)/shard_map/dot_general | solution.py:27
  122.8 5.2 %fusion.27 = bf16[4,256,512]{2,1,0:T(8,128)(2,1)} fusion(bf16[4,256,512]{2,1,0:T(8,128)(2,1)} %get-tuple-element.194, f32[4,256,512]{2,1,0:T(8,128)} %fusion.52, f32[4,256,512]{2,1,0:T(8,128)} %fusion.54, f32[4,256]{1,0:T(4,128)S(1)} %add_rsqrt_fusion.2, f32[512]{0:T(512)S(1)} %bitcast.185, bf16[4,3,512,512]{3,2,1,0:T(8,128)(2,1)} %all-gather.4.cloned.1.call-done, ...), kind=kOutput, calls=%fused_computation.65 | convolution fusion | flops 1081081856 | bytes 8394752 | tf_op jit(solution)/shard_map/dot_general | solution.py:33
  128.0 2.4 fusion.131
  131.0 3.2 %fusion.104 = f32[4,256,512]{2,1,0:T(8,128)} fusion(f32[512]{0:T(512)S(1)} %bitcast.192, f32[4,256]{1,0:T(4,128)S(1)} %add_rsqrt_fusion.7, bf16[4,3,512,512]{3,2,1,0:T(8,128)(2,1)} %all-gather.4.cloned.1.call-done, bf16[4,256,512]{2,1,0:T(8,128)(2,1)S(1)} %gather_fusion, pred[4]{0:T(512)(128)(4,1)S(1)} %get-tuple-element.210), kind=kOutput, calls=%fused_computation.135 | convolution fusion | flops 539492352 | bytes 3676164 | tf_op jit(solution)/shard_map/dot_general | solution.py:27
  134.2 3.1 %fusion.106 = f32[4,256,512]{2,1,0:T(8,128)} fusion(f32[512]{0:T(512)S(1)} %bitcast.193, f32[4,256]{1,0:T(4,128)S(1)} %add_rsqrt_fusion.7, bf16[4,3,512,512]{3,2,1,0:T(8,128)(2,1)} %all-gather.4.cloned.1.call-done, bf16[4,256,512]{2,1,0:T(8,128)(2,1)S(1)} %gather_fusion, pred[4]{0:T(512)(128)(4,1)S(1)} %get-tuple-element.210), kind=kOutput, calls=%fused_computation.136 | convolution fusion | flops 539492352 | bytes 3676164 | tf_op jit(solution)/shard_map/dot_general | solution.py:27
  137.3 4.6 %fusion.16 = (f32[4,256]{1,0:T(4,128)S(1)}, bf16[4,256,512]{2,1,0:T(8,128)(2,1)}) fusion(bf16[4,512,512]{2,1,0:T(8,128)(2,1)} %all-gather.6.cloned.1.call-done, f32[4,256,512]{2,1,0:T(8,128)} %fusion.104, f32[4,256,512]{2,1,0:T(8,128)} %fusion.106, f32[512]{0:T(512)S(1)} %bitcast.194, f32[4,256]{1,0:T(4,128)S(1)} %add_rsqrt_fusion.7, ...), kind=kOutput, calls=%fused_computation.54 | convolution fusion | flops 1083702272 | bytes 8399872 | tf_op jit(solution)/shard_map/dot_general | solution.py:33
  141.9 3.6 %fusion.82 = f32[4,256,512]{2,1,0:T(8,128)} fusion(bf16[4,256,512]{2,1,0:T(8,128)(2,1)} %get-tuple-element.196, f32[512]{0:T(512)S(1)} %bitcast.186, f32[4,256]{1,0:T(4,128)S(1)} %add_rsqrt_fusion.6, bf16[4,3,512,512]{3,2,1,0:T(8,128)(2,1)} %all-gather.4.cloned.1.call-done), kind=kOutput, calls=%fused_computation.119 | convolution fusion | flops 538968064 | bytes 3676160 | tf_op jit(solution)/shard_map/dot_general | solution.py:27
  145.5 3.1 %fusion.84 = f32[4,256,512]{2,1,0:T(8,128)} fusion(bf16[4,256,512]{2,1,0:T(8,128)(2,1)S(1)} %copy-done.15, f32[512]{0:T(512)S(1)} %bitcast.187, f32[4,256]{1,0:T(4,128)S(1)} %add_rsqrt_fusion.6, bf16[4,3,512,512]{3,2,1,0:T(8,128)(2,1)} %all-gather.4.cloned.1.call-done), kind=kOutput, calls=%fused_computation.120 | convolution fusion | flops 538968064 | bytes 3676160 | tf_op jit(solution)/shard_map/dot_general | solution.py:27
  148.7 4.3 %fusion.19 = bf16[4,256,512]{2,1,0:T(8,128)(2,1)S(1)} fusion(bf16[4,256,512]{2,1,0:T(8,128)(2,1)} %get-tuple-element.196, f32[4,256,512]{2,1,0:T(8,128)} %fusion.82, f32[4,256,512]{2,1,0:T(8,128)} %fusion.84, f32[512]{0:T(512)S(1)} %bitcast.188, f32[4,256]{1,0:T(4,128)S(1)} %add_rsqrt_fusion.6, bf16[4,3,512,512]{3,2,1,0:T(8,128)(2,1)} %all-gather.4.cloned.1.call-done, ...), kind=kOutput, calls=%fused_computation.57 | convolution fusion | flops 1081081856 | bytes 8394752 | tf_op jit(solution)/shard_map/dot_general | solution.py:33
  153.0 1.1 fusion.125
  155.3 0.7 broadcast_select_fusion.9
  156.3 6.6 %all-reduce.18 = (f32[8,18]{1,0:T(8,128)S(1)}, f32[8]{0:T(128)S(1)}) all-reduce(f32[8,18]{1,0:T(8,128)S(1)} %scatter-add.19, f32[8]{0:T(128)S(1)} %fusion.155), channel_id=1, replica_groups=mesh['section'=4,'dp_0'=4,'dp_1'=4,'dp_2'=2] {'section'}, use_global_device_ids=true, to_apply=%region_21.23 | all-reduce | flops 152 | bytes 1216 | tf_op jit(solution)/shard_map/psum | solution.py:16
  163.0 8.6 %all-reduce.17 = (f32[8,18]{1,0:T(8,128)S(1)}, f32[8]{0:T(128)S(1)}) all-reduce(f32[8,18]{1,0:T(8,128)S(1)} %get-tuple-element.167, f32[8]{0:T(128)S(1)} %get-tuple-element.168), channel_id=1, replica_groups=mesh['section'=4,'dp_0'=4,'dp_1'=4,'dp_2'=2] {'dp_0'}, use_global_device_ids=true, to_apply=%region_22.24 | all-reduce | flops 152 | bytes 1216 | tf_op jit(solution)/shard_map/psum | solution.py:16
  171.5 8.7 %all-reduce.16 = (f32[8,18]{1,0:T(8,128)S(1)}, f32[8]{0:T(128)S(1)}) all-reduce(f32[8,18]{1,0:T(8,128)S(1)} %get-tuple-element.165, f32[8]{0:T(128)S(1)} %get-tuple-element.166), channel_id=1, replica_groups=mesh['section'=4,'dp_0'=4,'dp_1'=4,'dp_2'=2] {'dp_1'}, use_global_device_ids=true, to_apply=%region_23.25 | all-reduce | flops 152 | bytes 1216 | tf_op jit(solution)/shard_map/psum | solution.py:16
  180.3 9.1 %all-reduce.19 = (f32[8,18]{1,0:T(8,128)S(1)}, f32[8]{0:T(128)S(1)}) all-reduce(f32[8,18]{1,0:T(8,128)S(1)} %get-tuple-element.163, f32[8]{0:T(128)S(1)} %get-tuple-element.164), channel_id=1, replica_groups=mesh['section'=4,'dp_0'=4,'dp_1'=4,'dp_2'=2] {'dp_2'}, use_global_device_ids=true, to_apply=%region_24.26 | all-reduce | flops 152 | bytes 1216 | tf_op jit(solution)/shard_map/psum | solution.py:16
  189.4 0.7 broadcast_select_fusion.11
  190.1 0.6 broadcast_select_fusion.8
  190.8 0.7 broadcast_select_fusion.7
  192.1 0.6 broadcast_select_fusion.5
  192.8 0.7 broadcast_select_fusion.4
  193.6 0.7 broadcast_select_fusion.3
  194.3 0.6 broadcast_select_fusion.2
  197.6 3.1 %fusion.120 = f32[4,256,512]{2,1,0:T(8,128)} fusion(bf16[4,256,512]{2,1,0:T(8,128)(2,1)S(1)} %bitcast.170, bf16[4,3,512,512]{3,2,1,0:T(8,128)(2,1)} %all-gather.4.cloned.1.call-done), kind=kOutput, calls=%fused_computation.160 | convolution fusion | flops 536870912 | bytes 3670016 | tf_op jit(solution)/shard_map/dot_general | solution.py:27
  200.7 3.1 %fusion.118 = f32[4,256,512]{2,1,0:T(8,128)} fusion(bf16[4,256,512]{2,1,0:T(8,128)(2,1)S(1)} %bitcast.171, bf16[4,3,512,512]{3,2,1,0:T(8,128)(2,1)} %all-gather.4.cloned.1.call-done), kind=kOutput, calls=%fused_computation.158 | convolution fusion | flops 536870912 | bytes 3670016 | tf_op jit(solution)/shard_map/dot_general | solution.py:27
  203.8 5.2 %fusion.28 = (f32[4,256]{1,0:T(4,128)S(1)}, bf16[4,256,512]{2,1,0:T(8,128)(2,1)}) fusion(f32[4,256,512]{2,1,0:T(8,128)} %bitcast.174, bf16[4,512,512]{2,1,0:T(8,128)(2,1)} %all-gather.6.cloned.1.call-done, f32[4,256,512]{2,1,0:T(8,128)} %fusion.120, f32[4,256,512]{2,1,0:T(8,128)} %fusion.118, bf16[4,256,512]{2,1,0:T(8,128)(2,1)S(1)} %bitcast.172, ...), kind=kOutput, calls=%fused_computation.66 | convolution fusion | flops 1080032256 | bytes 9441280 | tf_op jit(solution)/shard_map/dot_general | solution.py:33
  209.0 3.5 %fusion.48 = f32[4,256,512]{2,1,0:T(8,128)} fusion(bf16[4,256,512]{2,1,0:T(8,128)(2,1)} %get-tuple-element.202, f32[4,256]{1,0:T(4,128)S(1)} %add_rsqrt_fusion, f32[512]{0:T(512)S(1)} %bitcast.177, bf16[4,3,512,512]{3,2,1,0:T(8,128)(2,1)} %all-gather.4.cloned.1.call-done), kind=kOutput, calls=%fused_computation.103 | convolution fusion | flops 538968064 | bytes 3676160 | tf_op jit(solution)/shard_map/dot_general | solution.py:27
  212.5 3.2 %fusion.46 = f32[4,256,512]{2,1,0:T(8,128)} fusion(bf16[4,256,512]{2,1,0:T(8,128)(2,1)S(1)} %copy-done.14, f32[4,256]{1,0:T(4,128)S(1)} %add_rsqrt_fusion, f32[512]{0:T(512)S(1)} %bitcast.178, bf16[4,3,512,512]{3,2,1,0:T(8,128)(2,1)} %all-gather.4.cloned.1.call-done), kind=kOutput, calls=%fused_computation.102 | convolution fusion | flops 538968064 | bytes 3676160 | tf_op jit(solution)/shard_map/dot_general | solution.py:27
  215.7 3.8 %fusion.43 = f32[4,256]{1,0:T(4,128)S(1)} fusion(f32[4,256,512]{2,1,0:T(8,128)} %fusion.46, f32[4,256,512]{2,1,0:T(8,128)} %fusion.48, bf16[4,256,512]{2,1,0:T(8,128)(2,1)S(1)} %copy-done.14, f32[4,256]{1,0:T(4,128)S(1)} %add_rsqrt_fusion, f32[512]{0:T(512)S(1)} %bitcast.179, bf16[4,3,512,512]{3,2,1,0:T(8,128)(2,1)} %all-gather.4.cloned.1.call-done, ...), kind=kOutput, calls=%fused_computation.81 | convolution fusion | flops 1084226560 | bytes 8399360 | tf_op jit(solution)/shard_map/dot_general | solution.py:33
  219.5 3.0 %fusion.121 = f32[4,256,512]{2,1,0:T(8,128)} fusion(bf16[4,256,512]{2,1,0:T(8,128)(2,1)S(1)} %bitcast.167, bf16[4,3,512,512]{3,2,1,0:T(8,128)(2,1)} %all-gather.4.cloned.1.call-done), kind=kOutput, calls=%fused_computation.161 | convolution fusion | flops 536870912 | bytes 3670016 | tf_op jit(solution)/shard_map/dot_general | solution.py:27
  222.5 3.3 %fusion.119 = f32[4,256,512]{2,1,0:T(8,128)} fusion(bf16[4,256,512]{2,1,0:T(8,128)(2,1)S(1)} %bitcast.168, bf16[4,3,512,512]{3,2,1,0:T(8,128)(2,1)} %all-gather.4.cloned.1.call-done), kind=kOutput, calls=%fused_computation.159 | convolution fusion | flops 536870912 | bytes 3670016 | tf_op jit(solution)/shard_map/dot_general | solution.py:27
  225.8 4.4 %fusion.20 = (f32[4,256]{1,0:T(4,128)S(1)}, bf16[4,256,512]{2,1,0:T(8,128)(2,1)}) fusion(f32[4,256,512]{2,1,0:T(8,128)S(1)} %bitcast.173, bf16[4,512,512]{2,1,0:T(8,128)(2,1)} %all-gather.6.cloned.1.call-done, f32[4,256,512]{2,1,0:T(8,128)} %fusion.121, f32[4,256,512]{2,1,0:T(8,128)} %fusion.119, bf16[4,256,512]{2,1,0:T(8,128)(2,1)S(1)} %bitcast.169, ...), kind=kOutput, calls=%fused_computation.58 | convolution fusion | flops 1080032256 | bytes 9441280 | tf_op jit(solution)/shard_map/dot_general | solution.py:33
  230.2 3.6 %fusion.68 = f32[4,256,512]{2,1,0:T(8,128)} fusion(bf16[4,256,512]{2,1,0:T(8,128)(2,1)} %get-tuple-element.204, f32[512]{0:T(512)S(1)} %bitcast.180, f32[4,256]{1,0:T(4,128)S(1)} %add_rsqrt_fusion.4, bf16[4,3,512,512]{3,2,1,0:T(8,128)(2,1)} %all-gather.4.cloned.1.call-done), kind=kOutput, calls=%fused_computation.111 | convolution fusion | flops 538968064 | bytes 3676160 | tf_op jit(solution)/shard_map/dot_general | solution.py:27
  233.8 3.2 %fusion.70 = f32[4,256,512]{2,1,0:T(8,128)} fusion(bf16[4,256,512]{2,1,0:T(8,128)(2,1)S(1)} %copy-done.13, f32[512]{0:T(512)S(1)} %bitcast.181, f32[4,256]{1,0:T(4,128)S(1)} %add_rsqrt_fusion.4, bf16[4,3,512,512]{3,2,1,0:T(8,128)(2,1)} %all-gather.4.cloned.1.call-done), kind=kOutput, calls=%fused_computation.112 | convolution fusion | flops 538968064 | bytes 3676160 | tf_op jit(solution)/shard_map/dot_general | solution.py:27
  237.0 3.8 %fusion.37 = f32[4,256]{1,0:T(4,128)S(1)} fusion(f32[4,256,512]{2,1,0:T(8,128)} %fusion.68, f32[4,256,512]{2,1,0:T(8,128)} %fusion.70, bf16[4,256,512]{2,1,0:T(8,128)(2,1)S(1)} %copy-done.13, f32[512]{0:T(512)S(1)} %bitcast.182, f32[4,256]{1,0:T(4,128)S(1)} %add_rsqrt_fusion.4, bf16[4,3,512,512]{3,2,1,0:T(8,128)(2,1)} %all-gather.4.cloned.1.call-done, ...), kind=kOutput, calls=%fused_computation.75 | convolution fusion | flops 1084226560 | bytes 8399360 | tf_op jit(solution)/shard_map/dot_general | solution.py:33
  (78 shorter events, 6.8 us)
Async XLA Ops:
  7.2 187.9 %copy-start = (bf16[18,512]{1,0:T(8,128)(2,1)S(1)}, bf16[18,512]{1,0:T(8,128)(2,1)}, u32[]{:S(2)}) copy-start(bf16[18,512]{1,0:T(8,128)(2,1)} %param.43) | copy-start | bytes 55300
  7.2 1.5 copy-start.7
  7.2 12.6 %copy-start.8 = (s32[8,4]{0,1:T(4,128)S(1)}, s32[8,4]{0,1:T(4,128)}, u32[]{:S(2)}) copy-start(s32[8,4]{0,1:T(4,128)} %param.36) | copy-start | bytes 388
  7.2 71.3 %all-gather.4.cloned.1.call-start = ((), (), s32[]{:S(2)}) async-start(), calls=%async_computation | async-start | bytes 7864320 | tf_op jit(solution)/shard_map/all_gather | solution.py:97
  7.9 103.5 %all-gather.6.cloned.1.call-start = ((), (), s32[]{:S(2)}) async-start(), calls=%async_computation.1 | async-start | bytes 2621440 | tf_op jit(solution)/shard_map/all_gather | solution.py:98
  20.1 14.8 %copy-start.10 = (bf16[1,512]{1,0:T(2,128)(2,1)S(1)}, bf16[1,512]{1,0:T(2,128)(2,1)}, u32[]{:S(2)}) copy-start(bf16[1,512]{1,0:T(2,128)(2,1)} %param.40) | copy-start | bytes 3076
  20.1 25.6 %copy-start.9 = (s32[2]{0:T(128)S(1)}, s32[2]{0:T(128)}, u32[]{:S(2)}) copy-start(s32[2]{0:T(128)} %constant.322.clone.1) | copy-start | bytes 28
  24.8 112.5 %copy-start.5 = (bf16[4,256,512]{2,1,0:T(8,128)(2,1)}, bf16[4,256,512]{2,1,0:T(8,128)(2,1)S(1)}, u32[]{:S(2)}) copy-start(bf16[4,256,512]{2,1,0:T(8,128)(2,1)S(1)} %gather_fusion) | copy-start | bytes 3145732
  116.1 3.5 %copy-start.16 = (bf16[4,256,512]{2,1,0:T(8,128)(2,1)S(1)}, bf16[4,256,512]{2,1,0:T(8,128)(2,1)}, u32[]{:S(2)}) copy-start(bf16[4,256,512]{2,1,0:T(8,128)(2,1)} %get-tuple-element.194) | copy-start | bytes 3145732
  122.8 5.2 %copy-start.11 = (bf16[512,18]{0,1:T(8,128)(2,1)S(1)}, bf16[512,18]{0,1:T(8,128)(2,1)}, u32[]{:S(2)}) copy-start(bf16[512,18]{0,1:T(8,128)(2,1)} %param.41) | copy-start | bytes 55300
  122.8 5.2 %copy-start.12 = (f32[18]{0:T(128)S(1)}, f32[18]{0:T(128)}, u32[]{:S(2)}) copy-start(f32[18]{0:T(128)} %param.42) | copy-start | bytes 220
  141.9 3.6 %copy-start.15 = (bf16[4,256,512]{2,1,0:T(8,128)(2,1)S(1)}, bf16[4,256,512]{2,1,0:T(8,128)(2,1)}, u32[]{:S(2)}) copy-start(bf16[4,256,512]{2,1,0:T(8,128)(2,1)} %get-tuple-element.196) | copy-start | bytes 3145732
  195.7 1.4 copy-start.2
  196.2 1.4 copy-start.4
  209.0 3.5 %copy-start.14 = (bf16[4,256,512]{2,1,0:T(8,128)(2,1)S(1)}, bf16[4,256,512]{2,1,0:T(8,128)(2,1)}, u32[]{:S(2)}) copy-start(bf16[4,256,512]{2,1,0:T(8,128)(2,1)} %get-tuple-element.202) | copy-start | bytes 3145732
  222.5 3.3 %copy-start.3 = (f32[1024,512]{1,0:T(8,128)S(1)}, f32[1024,512]{1,0:T(8,128)}, u32[]{:S(2)}) copy-start(f32[1024,512]{1,0:T(8,128)} %copy-done.2) | copy-start | bytes 6291460
  230.2 3.6 %copy-start.13 = (bf16[4,256,512]{2,1,0:T(8,128)(2,1)S(1)}, bf16[4,256,512]{2,1,0:T(8,128)(2,1)}, u32[]{:S(2)}) copy-start(bf16[4,256,512]{2,1,0:T(8,128)(2,1)} %get-tuple-element.204) | copy-start | bytes 3145732
  233.8 3.2 %copy-start.6 = (bf16[4,256,512]{2,1,0:T(8,128)(2,1)S(1)}, bf16[4,256,512]{2,1,0:T(8,128)(2,1)}, u32[]{:S(2)}) copy-start(bf16[4,256,512]{2,1,0:T(8,128)(2,1)} %copy-done.5) | copy-start | bytes 3145732
  237.0 4.9 %copy-start.1 = (bf16[18,512]{1,0:T(8,128)(2,1)S(1)}, bf16[18,512]{1,0:T(8,128)(2,1)}, u32[]{:S(2)}) copy-start(bf16[18,512]{1,0:T(8,128)(2,1)} %param.43) | copy-start | bytes 55300
Sparse Core Ops, SparseCore 0:
  9.7 68.7 all-gather.3
  80.1 31.2 all-gather.5
where the time goes:
time: 250 us; the launch traced here: 249 us
  matrix products  92.5 us (37%)
  waiting for transfers between devices  58.3 us (23%)
  blocking collectives  43.8 us (18%)
  between operations  31.2 us (12%)
  local copies, waits for them, and re-layouts  11.8 us (5%)
  other arithmetic  11.1 us (4%)
    dot_general x16, matrix products, run_block(): jnp.dot(flat, tap_set[k], preferred_element_type=jnp.float32)  52 us
    dot_general x8, matrix products, run_block(): jnp.dot(activated.reshape(-1, channels), out_weight, preferred_element_ty...  35.9 us
    psum x4, blocking collectives, over_axes(): return functools.reduce(lax.psum, axes, array)  33 us
    all_gather x1, waiting for transfers between devices, on_device(): lax.all_gather(tap_weights, 'section', axis=0, tiled=True)  30.2 us
    all_gather x1, waiting for transfers between devices, on_device(): lax.all_gather(out_weights, 'section', axis=0, tiled=True)  26.6 us
    all_gather x1, blocking collectives, on_device(): lax.all_gather(norm_gains, 'section', axis=0, tiled=True)  10.8 us
    gather x2, local copies, waits for them, and re-layouts, on_device(): source = jnp.take(clip_pool, clip_index[batch_slot], axis=0)  9.48 us
    another operation x12, other arithmetic  8.18 us
  transfers between devices with their start and end apart: 2, of which 2 were waited for; matrix products, arithmetic and copies ran while one was open for 8% of the time, Pallas kernels for 0%

commit v1 on v0

--- a/solution.py
+++ b/solution.py
@@ -10,6 +10,12 @@
 SECTION_DP = ("section", "dp_0", "dp_1", "dp_2")
 norm_eps = 1e-06
 quant_section = 1
+
+
+def tiled_gather(x, axis, dim):
+    size = lax.axis_size(axis)
+    repeats = [size if d == dim else 1 for d in range(x.ndim)]
+    return lax.all_to_all(jnp.tile(x, repeats), axis, split_axis=dim, concat_axis=dim, tiled=True)
 
 
 def over_axes(array, axes):
@@ -94,7 +100,7 @@
     bit_buffer = jnp.zeros((batches, quant_weight.shape[1]), jnp.float32)
     entropy_buffer = jnp.zeros((batches,), jnp.float32)
     all_taps, all_out, all_gains = (
-        lax.all_gather(tap_weights, "section", axis=0, tiled=True),
+        tiled_gather(tap_weights, "section", 0),
         lax.all_gather(out_weights, "section", axis=0, tiled=True),
         lax.all_gather(norm_gains, "section", axis=0, tiled=True),
     )

time: 250 us -> 261 us (1.044)
  blocking collectives: 43.8 us -> 103 us
  waiting for transfers between devices: 58.3 us -> 0.68 us
  starting transfers between devices: 0.08 us -> 5.41 us
  local copies, waits for them, and re-layouts: 11.8 us -> 15.5 us
    all_gather x1, blocking collectives: 10.8 us -> 65.1 us  [on_device(): lax.all_gather(norm_gains, 'section', axis=0, tiled=True)]
    all_gather x1 -> x0, waiting for transfers between devices: 30.2 us -> none  [on_device(): lax.all_gather(tap_weights, 'section', axis=0, tiled=True)]
    all_gather x1, waiting for transfers between devices: 26.6 us -> 0.01 us  [on_device(): lax.all_gather(out_weights, 'section', axis=0, tiled=True)]
    all_to_all x0 -> x1, starting transfers between devices: none -> 5.37 us  [tiled_gather(): lax.all_to_all(jnp.tile(x, repeats), axis, split_axis=dim, concat_axis=di...]
    another operation x3 -> x4, local copies, waits for them, and re-layouts: 0.01 us -> 4.62 us  [the longest x1 4.61 us: tiled_gather(): jnp.tile(x, repeats)]
    psum x4, blocking collectives: 33 us -> 37.6 us  [over_axes(): return functools.reduce(lax.psum, axes, array)]
  transfers between devices with their start and end apart: 2 -> 2, of which waited for: 2 -> 0; matrix products, arithmetic and copies ran while one was open for 8% -> 7% of each run, Pallas kernels for 0% -> 0%
where the time goes in v1:
time: 261 us; the launch traced here: 259 us
  blocking collectives  103 us (39%)
  matrix products  92.6 us (35%)
  between operations  31.1 us (12%)
  local copies, waits for them, and re-layouts  15.5 us (6%)
  other arithmetic  11.1 us (4%)
  starting transfers between devices  5.41 us (2%)
    all_gather x1, blocking collectives, on_device(): lax.all_gather(norm_gains, 'section', axis=0, tiled=True)  65.1 us
    dot_general x16, matrix products, run_block(): jnp.dot(flat, tap_set[k], preferred_element_type=jnp.float32)  52.3 us
    psum x4, blocking collectives, over_axes(): return functools.reduce(lax.psum, axes, array)  37.6 us
    dot_general x8, matrix products, run_block(): jnp.dot(activated.reshape(-1, channels), out_weight, preferred_element_ty...  35.7 us
    gather x2, local copies, waits for them, and re-layouts, on_device(): source = jnp.take(clip_pool, clip_index[batch_slot], axis=0)  8.58 us
    another operation x12, other arithmetic  8.18 us
    all_to_all x1, starting transfers between devices, tiled_gather(): lax.all_to_all(jnp.tile(x, repeats), axis, split_axis=dim, concat_axis=di...  5.37 us
  transfers between devices with their start and end apart: 2, of which 0 were waited for; matrix products, arithmetic and copies ran while one was open for 7% of the time, Pallas kernels for 0%

profile of v1, /device:TPU:1, one launch (start us, length us, event | category | flops | bytes accessed | tf_op | source)
XLA Modules:
  0.0 259.1 jit_solution(2954076883967541740)
XLA Ops:
  7.2 4.6 %tile.10 = bf16[4,3,512,512]{3,2,1,0:T(8,128)(2,1)} broadcast(bf16[3,512,512]{2,1,0:T(8,128)(2,1)} %bitcast.176), dimensions={1,2,3} | broadcast | bytes 7864320 | tf_op jit(solution)/shard_map/tile | solution.py:18
  11.8 5.4 %all-to-all-start = ((bf16[4,3,512,512]{3,2,1,0:T(8,128)(2,1)}), bf16[4,3,512,512]{3,2,1,0:T(8,128)(2,1)}, u32[]{:S(2)}, u32[]{:S(2)}) async-start(bf16[4,3,512,512]{3,2,1,0:T(8,128)(2,1)} %tile.10), calls=%async_computation | async-start | bytes 12582912 | tf_op jit(solution)/shard_map/all_to_all | solution.py:18
  17.2 0.7 all-gather.3.cloned.1.call-update
  17.9 0.7 fusion.181
  29.2 4.1 %gather_fusion = bf16[4,256,512]{2,1,0:T(8,128)(2,1)S(1)} fusion(bf16[32,256,512]{2,1,0:T(8,128)(2,1)} %param.35, s32[1024]{0:T(1024)S(1)} %pad_clamp_fusion.1), kind=kCustom, calls=%fused_computation.clone | custom fusion | bytes 2097168 | tf_op jit(solution)/shard_map/jit(_take)/gather | solution.py:111
  33.3 4.5 %gather_fusion.1 = bf16[4,256,512]{2,1,0:T(8,128)(2,1)S(1)} fusion(bf16[32,256,512]{2,1,0:T(8,128)(2,1)} %param.35, s32[1024]{0:T(1024)S(1)} %pad_clamp_fusion), kind=kCustom, calls=%fused_computation.1.clone | custom fusion | bytes 2097168 | tf_op jit(solution)/shard_map/jit(_take)/gather | solution.py:111
  43.0 65.1 %all-gather = bf16[4,1,512]{2,1,0:T(2,128)(2,1)S(1)} all-gather(bf16[1,1,512]{2,1,0:T(2,128)(2,1)S(1)} %bitcast.178), channel_id=1, replica_groups=mesh['section'=4,'dp_0'=4,'dp_1'=4,'dp_2'=2] {'section'}, dimensions={0}, use_global_device_ids=true | all-gather | bytes 5120 | tf_op jit(solution)/shard_map/all_gather | solution.py:105
  108.1 0.8 and_reduce_fusion.4
  108.9 0.9 and_reduce_fusion
  110.7 3.2 %fusion.58 = f32[4,256,512]{2,1,0:T(8,128)} fusion(f32[4,256]{1,0:T(4,128)S(1)} %add_rsqrt_fusion.3, f32[512]{0:T(512)S(1)} %bitcast.191, bf16[4,3,512,512]{3,2,1,0:T(8,128)(2,1)} %all-to-all-done, bf16[4,256,512]{2,1,0:T(8,128)(2,1)S(1)} %gather_fusion.1, pred[4]{0:T(512)(128)(4,1)S(1)} %get-tuple-element.209), kind=kOutput, calls=%fused_computation.106 | convolution fusion | flops 539492352 | bytes 3676164 | tf_op jit(solution)/shard_map/dot_general | solution.py:33
  113.8 3.2 %fusion.60 = f32[4,256,512]{2,1,0:T(8,128)} fusion(f32[4,256]{1,0:T(4,128)S(1)} %add_rsqrt_fusion.3, f32[512]{0:T(512)S(1)} %bitcast.192, bf16[4,3,512,512]{3,2,1,0:T(8,128)(2,1)} %all-to-all-done, bf16[4,256,512]{2,1,0:T(8,128)(2,1)S(1)} %gather_fusion.1, pred[4]{0:T(512)(128)(4,1)S(1)} %get-tuple-element.209), kind=kOutput, calls=%fused_computation.107 | convolution fusion | flops 539492352 | bytes 3676164 | tf_op jit(solution)/shard_map/dot_general | solution.py:33
  117.0 4.5 %fusion.24 = (f32[4,256]{1,0:T(4,128)S(1)}, bf16[4,256,512]{2,1,0:T(8,128)(2,1)}) fusion(bf16[4,512,512]{2,1,0:T(8,128)(2,1)} %all-gather.3.cloned.1.call-done, f32[4,256,512]{2,1,0:T(8,128)} %fusion.58, f32[4,256,512]{2,1,0:T(8,128)} %fusion.60, f32[4,256]{1,0:T(4,128)S(1)} %add_rsqrt_fusion.3, f32[512]{0:T(512)S(1)} %bitcast.193, ...), kind=kOutput, calls=%fused_computation.62 | convolution fusion | flops 1083702272 | bytes 8399872 | tf_op jit(solution)/shard_map/dot_general | solution.py:39
  121.6 3.6 %fusion.54 = f32[4,256,512]{2,1,0:T(8,128)} fusion(bf16[4,256,512]{2,1,0:T(8,128)(2,1)} %get-tuple-element.194, f32[4,256]{1,0:T(4,128)S(1)} %add_rsqrt_fusion.2, f32[512]{0:T(512)S(1)} %bitcast.185, bf16[4,3,512,512]{3,2,1,0:T(8,128)(2,1)} %all-to-all-done), kind=kOutput, calls=%fused_computation.105 | convolution fusion | flops 538968064 | bytes 3676160 | tf_op jit(solution)/shard_map/dot_general | solution.py:33
  125.2 3.2 %fusion.52 = f32[4,256,512]{2,1,0:T(8,128)} fusion(bf16[4,256,512]{2,1,0:T(8,128)(2,1)S(1)} %copy-done.16, f32[4,256]{1,0:T(4,128)S(1)} %add_rsqrt_fusion.2, f32[512]{0:T(512)S(1)} %bitcast.186, bf16[4,3,512,512]{3,2,1,0:T(8,128)(2,1)} %all-to-all-done), kind=kOutput, calls=%fused_computation.104 | convolution fusion | flops 538968064 | bytes 3676160 | tf_op jit(solution)/shard_map/dot_general | solution.py:33
  128.4 5.2 %fusion.27 = bf16[4,256,512]{2,1,0:T(8,128)(2,1)} fusion(bf16[4,256,512]{2,1,0:T(8,128)(2,1)} %get-tuple-element.194, f32[4,256,512]{2,1,0:T(8,128)} %fusion.52, f32[4,256,512]{2,1,0:T(8,128)} %fusion.54, f32[4,256]{1,0:T(4,128)S(1)} %add_rsqrt_fusion.2, f32[512]{0:T(512)S(1)} %bitcast.187, bf16[4,3,512,512]{3,2,1,0:T(8,128)(2,1)} %all-to-all-done, ...), kind=kOutput, calls=%fused_computation.65 | convolution fusion | flops 1081081856 | bytes 8394752 | tf_op jit(solution)/shard_map/dot_general | solution.py:39
  133.5 2.4 fusion.131
  136.6 3.2 %fusion.104 = f32[4,256,512]{2,1,0:T(8,128)} fusion(f32[512]{0:T(512)S(1)} %bitcast.194, f32[4,256]{1,0:T(4,128)S(1)} %add_rsqrt_fusion.7, bf16[4,3,512,512]{3,2,1,0:T(8,128)(2,1)} %all-to-all-done, bf16[4,256,512]{2,1,0:T(8,128)(2,1)S(1)} %gather_fusion, pred[4]{0:T(512)(128)(4,1)S(1)} %get-tuple-element.210), kind=kOutput, calls=%fused_computation.135 | convolution fusion | flops 539492352 | bytes 3676164 | tf_op jit(solution)/shard_map/dot_general | solution.py:33
  139.7 3.2 %fusion.106 = f32[4,256,512]{2,1,0:T(8,128)} fusion(f32[512]{0:T(512)S(1)} %bitcast.195, f32[4,256]{1,0:T(4,128)S(1)} %add_rsqrt_fusion.7, bf16[4,3,512,512]{3,2,1,0:T(8,128)(2,1)} %all-to-all-done, bf16[4,256,512]{2,1,0:T(8,128)(2,1)S(1)} %gather_fusion, pred[4]{0:T(512)(128)(4,1)S(1)} %get-tuple-element.210), kind=kOutput, calls=%fused_computation.136 | convolution fusion | flops 539492352 | bytes 3676164 | tf_op jit(solution)/shard_map/dot_general | solution.py:33
  142.9 4.5 %fusion.16 = (f32[4,256]{1,0:T(4,128)S(1)}, bf16[4,256,512]{2,1,0:T(8,128)(2,1)}) fusion(bf16[4,512,512]{2,1,0:T(8,128)(2,1)} %all-gather.3.cloned.1.call-done, f32[4,256,512]{2,1,0:T(8,128)} %fusion.104, f32[4,256,512]{2,1,0:T(8,128)} %fusion.106, f32[512]{0:T(512)S(1)} %bitcast.196, f32[4,256]{1,0:T(4,128)S(1)} %add_rsqrt_fusion.7, ...), kind=kOutput, calls=%fused_computation.54 | convolution fusion | flops 1083702272 | bytes 8399872 | tf_op jit(solution)/shard_map/dot_general | solution.py:39
  147.5 3.5 %fusion.82 = f32[4,256,512]{2,1,0:T(8,128)} fusion(bf16[4,256,512]{2,1,0:T(8,128)(2,1)} %get-tuple-element.196, f32[512]{0:T(512)S(1)} %bitcast.188, f32[4,256]{1,0:T(4,128)S(1)} %add_rsqrt_fusion.6, bf16[4,3,512,512]{3,2,1,0:T(8,128)(2,1)} %all-to-all-done), kind=kOutput, calls=%fused_computation.119 | convolution fusion | flops 538968064 | bytes 3676160 | tf_op jit(solution)/shard_map/dot_general | solution.py:33
  151.0 3.2 %fusion.84 = f32[4,256,512]{2,1,0:T(8,128)} fusion(bf16[4,256,512]{2,1,0:T(8,128)(2,1)S(1)} %copy-done.15, f32[512]{0:T(512)S(1)} %bitcast.189, f32[4,256]{1,0:T(4,128)S(1)} %add_rsqrt_fusion.6, bf16[4,3,512,512]{3,2,1,0:T(8,128)(2,1)} %all-to-all-done), kind=kOutput, calls=%fused_computation.120 | convolution fusion | flops 538968064 | bytes 3676160 | tf_op jit(solution)/shard_map/dot_general | solution.py:33
  154.2 4.3 %fusion.19 = bf16[4,256,512]{2,1,0:T(8,128)(2,1)S(1)} fusion(bf16[4,256,512]{2,1,0:T(8,128)(2,1)} %get-tuple-element.196, f32[4,256,512]{2,1,0:T(8,128)} %fusion.82, f32[4,256,512]{2,1,0:T(8,128)} %fusion.84, f32[512]{0:T(512)S(1)} %bitcast.190, f32[4,256]{1,0:T(4,128)S(1)} %add_rsqrt_fusion.6, bf16[4,3,512,512]{3,2,1,0:T(8,128)(2,1)} %all-to-all-done, ...), kind=kOutput, calls=%fused_computation.57 | convolution fusion | flops 1081081856 | bytes 8394752 | tf_op jit(solution)/shard_map/dot_general | solution.py:39
  158.6 1.1 fusion.125
  161.0 0.7 broadcast_select_fusion.9
  162.0 7.3 %all-reduce.18 = (f32[8,18]{1,0:T(8,128)S(1)}, f32[8]{0:T(128)S(1)}) all-reduce(f32[8,18]{1,0:T(8,128)S(1)} %scatter-add.19, f32[8]{0:T(128)S(1)} %fusion.155), channel_id=1, replica_groups=mesh['section'=4,'dp_0'=4,'dp_1'=4,'dp_2'=2] {'section'}, use_global_device_ids=true, to_apply=%region_21.23 | all-reduce | flops 152 | bytes 1216 | tf_op jit(solution)/shard_map/psum | solution.py:22
  169.3 9.2 %all-reduce.17 = (f32[8,18]{1,0:T(8,128)S(1)}, f32[8]{0:T(128)S(1)}) all-reduce(f32[8,18]{1,0:T(8,128)S(1)} %get-tuple-element.167, f32[8]{0:T(128)S(1)} %get-tuple-element.168), channel_id=1, replica_groups=mesh['section'=4,'dp_0'=4,'dp_1'=4,'dp_2'=2] {'dp_0'}, use_global_device_ids=true, to_apply=%region_22.24 | all-reduce | flops 152 | bytes 1216 | tf_op jit(solution)/shard_map/psum | solution.py:22
  178.5 9.8 %all-reduce.16 = (f32[8,18]{1,0:T(8,128)S(1)}, f32[8]{0:T(128)S(1)}) all-reduce(f32[8,18]{1,0:T(8,128)S(1)} %get-tuple-element.165, f32[8]{0:T(128)S(1)} %get-tuple-element.166), channel_id=1, replica_groups=mesh['section'=4,'dp_0'=4,'dp_1'=4,'dp_2'=2] {'dp_1'}, use_global_device_ids=true, to_apply=%region_23.25 | all-reduce | flops 152 | bytes 1216 | tf_op jit(solution)/shard_map/psum | solution.py:22
  188.4 11.2 %all-reduce.19 = (f32[8,18]{1,0:T(8,128)S(1)}, f32[8]{0:T(128)S(1)}) all-reduce(f32[8,18]{1,0:T(8,128)S(1)} %get-tuple-element.163, f32[8]{0:T(128)S(1)} %get-tuple-element.164), channel_id=1, replica_groups=mesh['section'=4,'dp_0'=4,'dp_1'=4,'dp_2'=2] {'dp_2'}, use_global_device_ids=true, to_apply=%region_24.26 | all-reduce | flops 152 | bytes 1216 | tf_op jit(solution)/shard_map/psum | solution.py:22
  199.6 0.7 broadcast_select_fusion.11
  200.4 0.6 broadcast_select_fusion.8
  201.1 0.7 broadcast_select_fusion.7
  202.4 0.6 broadcast_select_fusion.5
  203.1 0.7 broadcast_select_fusion.4
  203.8 0.7 broadcast_select_fusion.3
  204.6 0.6 broadcast_select_fusion.2
  207.3 0.7 copy-done.4
  208.0 3.0 %fusion.120 = f32[4,256,512]{2,1,0:T(8,128)} fusion(bf16[4,256,512]{2,1,0:T(8,128)(2,1)S(1)} %bitcast.171, bf16[4,3,512,512]{3,2,1,0:T(8,128)(2,1)} %all-to-all-done), kind=kOutput, calls=%fused_computation.160 | convolution fusion | flops 536870912 | bytes 3670016 | tf_op jit(solution)/shard_map/dot_general | solution.py:33
  211.0 3.1 %fusion.118 = f32[4,256,512]{2,1,0:T(8,128)} fusion(bf16[4,256,512]{2,1,0:T(8,128)(2,1)S(1)} %bitcast.172, bf16[4,3,512,512]{3,2,1,0:T(8,128)(2,1)} %all-to-all-done), kind=kOutput, calls=%fused_computation.158 | convolution fusion | flops 536870912 | bytes 3670016 | tf_op jit(solution)/shard_map/dot_general | solution.py:33
  214.1 5.2 %fusion.28 = (f32[4,256]{1,0:T(4,128)S(1)}, bf16[4,256,512]{2,1,0:T(8,128)(2,1)}) fusion(f32[4,256,512]{2,1,0:T(8,128)} %bitcast.175, bf16[4,512,512]{2,1,0:T(8,128)(2,1)} %all-gather.3.cloned.1.call-done, f32[4,256,512]{2,1,0:T(8,128)} %fusion.120, f32[4,256,512]{2,1,0:T(8,128)} %fusion.118, bf16[4,256,512]{2,1,0:T(8,128)(2,1)S(1)} %bitcast.173, ...), kind=kOutput, calls=%fused_computation.66 | convolution fusion | flops 1080032256 | bytes 9441280 | tf_op jit(solution)/shard_map/dot_general | solution.py:39
  219.3 3.6 %fusion.48 = f32[4,256,512]{2,1,0:T(8,128)} fusion(bf16[4,256,512]{2,1,0:T(8,128)(2,1)} %get-tuple-element.202, f32[4,256]{1,0:T(4,128)S(1)} %add_rsqrt_fusion, f32[512]{0:T(512)S(1)} %bitcast.179, bf16[4,3,512,512]{3,2,1,0:T(8,128)(2,1)} %all-to-all-done), kind=kOutput, calls=%fused_computation.103 | convolution fusion | flops 538968064 | bytes 3676160 | tf_op jit(solution)/shard_map/dot_general | solution.py:33
  222.9 3.1 %fusion.46 = f32[4,256,512]{2,1,0:T(8,128)} fusion(bf16[4,256,512]{2,1,0:T(8,128)(2,1)S(1)} %copy-done.14, f32[4,256]{1,0:T(4,128)S(1)} %add_rsqrt_fusion, f32[512]{0:T(512)S(1)} %bitcast.180, bf16[4,3,512,512]{3,2,1,0:T(8,128)(2,1)} %all-to-all-done), kind=kOutput, calls=%fused_computation.102 | convolution fusion | flops 538968064 | bytes 3676160 | tf_op jit(solution)/shard_map/dot_general | solution.py:33
  226.0 3.8 %fusion.43 = f32[4,256]{1,0:T(4,128)S(1)} fusion(f32[4,256,512]{2,1,0:T(8,128)} %fusion.46, f32[4,256,512]{2,1,0:T(8,128)} %fusion.48, bf16[4,256,512]{2,1,0:T(8,128)(2,1)S(1)} %copy-done.14, f32[4,256]{1,0:T(4,128)S(1)} %add_rsqrt_fusion, f32[512]{0:T(512)S(1)} %bitcast.181, bf16[4,3,512,512]{3,2,1,0:T(8,128)(2,1)} %all-to-all-done, ...), kind=kOutput, calls=%fused_computation.81 | convolution fusion | flops 1084226560 | bytes 8399360 | tf_op jit(solution)/shard_map/dot_general | solution.py:39
  229.8 3.1 %fusion.121 = f32[4,256,512]{2,1,0:T(8,128)} fusion(bf16[4,256,512]{2,1,0:T(8,128)(2,1)S(1)} %bitcast.168, bf16[4,3,512,512]{3,2,1,0:T(8,128)(2,1)} %all-to-all-done), kind=kOutput, calls=%fused_computation.161 | convolution fusion | flops 536870912 | bytes 3670016 | tf_op jit(solution)/shard_map/dot_general | solution.py:33
  232.9 3.2 %fusion.119 = f32[4,256,512]{2,1,0:T(8,128)} fusion(bf16[4,256,512]{2,1,0:T(8,128)(2,1)S(1)} %bitcast.169, bf16[4,3,512,512]{3,2,1,0:T(8,128)(2,1)} %all-to-all-done), kind=kOutput, calls=%fused_computation.159 | convolution fusion | flops 536870912 | bytes 3670016 | tf_op jit(solution)/shard_map/dot_general | solution.py:33
  236.1 4.4 %fusion.20 = (f32[4,256]{1,0:T(4,128)S(1)}, bf16[4,256,512]{2,1,0:T(8,128)(2,1)}) fusion(f32[4,256,512]{2,1,0:T(8,128)S(1)} %bitcast.174, bf16[4,512,512]{2,1,0:T(8,128)(2,1)} %all-gather.3.cloned.1.call-done, f32[4,256,512]{2,1,0:T(8,128)} %fusion.121, f32[4,256,512]{2,1,0:T(8,128)} %fusion.119, bf16[4,256,512]{2,1,0:T(8,128)(2,1)S(1)} %bitcast.170, ...), kind=kOutput, calls=%fused_computation.58 | convolution fusion | flops 1080032256 | bytes 9441280 | tf_op jit(solution)/shard_map/dot_general | solution.py:39
  240.5 3.6 %fusion.68 = f32[4,256,512]{2,1,0:T(8,128)} fusion(bf16[4,256,512]{2,1,0:T(8,128)(2,1)} %get-tuple-element.204, f32[512]{0:T(512)S(1)} %bitcast.182, f32[4,256]{1,0:T(4,128)S(1)} %add_rsqrt_fusion.4, bf16[4,3,512,512]{3,2,1,0:T(8,128)(2,1)} %all-to-all-done), kind=kOutput, calls=%fused_computation.111 | convolution fusion | flops 538968064 | bytes 3676160 | tf_op jit(solution)/shard_map/dot_general | solution.py:33
  244.1 3.3 %fusion.70 = f32[4,256,512]{2,1,0:T(8,128)} fusion(bf16[4,256,512]{2,1,0:T(8,128)(2,1)S(1)} %copy-done.13, f32[512]{0:T(512)S(1)} %bitcast.183, f32[4,256]{1,0:T(4,128)S(1)} %add_rsqrt_fusion.4, bf16[4,3,512,512]{3,2,1,0:T(8,128)(2,1)} %all-to-all-done), kind=kOutput, calls=%fused_computation.112 | convolution fusion | flops 538968064 | bytes 3676160 | tf_op jit(solution)/shard_map/dot_general | solution.py:33
  247.4 3.7 %fusion.37 = f32[4,256]{1,0:T(4,128)S(1)} fusion(f32[4,256,512]{2,1,0:T(8,128)} %fusion.68, f32[4,256,512]{2,1,0:T(8,128)} %fusion.70, bf16[4,256,512]{2,1,0:T(8,128)(2,1)S(1)} %copy-done.13, f32[512]{0:T(512)S(1)} %bitcast.184, f32[4,256]{1,0:T(4,128)S(1)} %add_rsqrt_fusion.4, bf16[4,3,512,512]{3,2,1,0:T(8,128)(2,1)} %all-to-all-done, ...), kind=kOutput, calls=%fused_computation.75 | convolution fusion | flops 1084226560 | bytes 8399360 | tf_op jit(solution)/shard_map/dot_general | solution.py:39
  (78 shorter events, 6.2 us)
Async XLA Ops:
  7.2 198.2 %copy-start = (bf16[18,512]{1,0:T(8,128)(2,1)S(1)}, bf16[18,512]{1,0:T(8,128)(2,1)}, u32[]{:S(2)}) copy-start(bf16[18,512]{1,0:T(8,128)(2,1)} %param.43) | copy-start | bytes 55300
  11.8 6.1 %copy-start.7 = (s32[8]{0:T(128)S(1)}, s32[8]{0:T(128)}, u32[]{:S(2)}) copy-start(s32[8]{0:T(128)} %param.37) | copy-start | bytes 100
  11.8 17.1 %copy-start.8 = (s32[8,4]{0,1:T(4,128)S(1)}, s32[8,4]{0,1:T(4,128)}, u32[]{:S(2)}) copy-start(s32[8,4]{0,1:T(4,128)} %param.36) | copy-start | bytes 388
  11.8 98.9 %all-to-all-start = ((bf16[4,3,512,512]{3,2,1,0:T(8,128)(2,1)}), bf16[4,3,512,512]{3,2,1,0:T(8,128)(2,1)}, u32[]{:S(2)}, u32[]{:S(2)}) async-start(bf16[4,3,512,512]{3,2,1,0:T(8,128)(2,1)} %tile.10), calls=%async_computation | async-start | bytes 12582912 | tf_op jit(solution)/shard_map/all_to_all | solution.py:18
  17.2 99.9 %all-gather.3.cloned.1.call-start = ((), (), s32[]{:S(2)}) async-start(), calls=%async_computation.1 | async-start | bytes 2621440 | tf_op jit(solution)/shard_map/all_gather | solution.py:104
  29.2 13.8 %copy-start.10 = (bf16[1,512]{1,0:T(2,128)(2,1)S(1)}, bf16[1,512]{1,0:T(2,128)(2,1)}, u32[]{:S(2)}) copy-start(bf16[1,512]{1,0:T(2,128)(2,1)} %param.40) | copy-start | bytes 3076
  29.2 78.9 %copy-start.9 = (s32[2]{0:T(128)S(1)}, s32[2]{0:T(128)}, u32[]{:S(2)}) copy-start(s32[2]{0:T(128)} %constant.322.clone.1) | copy-start | bytes 28
  33.3 109.6 %copy-start.5 = (bf16[4,256,512]{2,1,0:T(8,128)(2,1)}, bf16[4,256,512]{2,1,0:T(8,128)(2,1)S(1)}, u32[]{:S(2)}) copy-start(bf16[4,256,512]{2,1,0:T(8,128)(2,1)S(1)} %gather_fusion) | copy-start | bytes 3145732
  121.6 3.6 %copy-start.16 = (bf16[4,256,512]{2,1,0:T(8,128)(2,1)S(1)}, bf16[4,256,512]{2,1,0:T(8,128)(2,1)}, u32[]{:S(2)}) copy-start(bf16[4,256,512]{2,1,0:T(8,128)(2,1)} %get-tuple-element.194) | copy-start | bytes 3145732
  128.4 5.2 %copy-start.11 = (bf16[512,18]{0,1:T(8,128)(2,1)S(1)}, bf16[512,18]{0,1:T(8,128)(2,1)}, u32[]{:S(2)}) copy-start(bf16[512,18]{0,1:T(8,128)(2,1)} %param.41) | copy-start | bytes 55300
  128.4 5.2 %copy-start.12 = (f32[18]{0:T(128)S(1)}, f32[18]{0:T(128)}, u32[]{:S(2)}) copy-start(f32[18]{0:T(128)} %param.42) | copy-start | bytes 220
  147.5 3.6 %copy-start.15 = (bf16[4,256,512]{2,1,0:T(8,128)(2,1)S(1)}, bf16[4,256,512]{2,1,0:T(8,128)(2,1)}, u32[]{:S(2)}) copy-start(bf16[4,256,512]{2,1,0:T(8,128)(2,1)} %get-tuple-element.196) | copy-start | bytes 3145732
  205.9 1.3 copy-start.2
  206.5 1.5 copy-start.4
  219.3 3.6 %copy-start.14 = (bf16[4,256,512]{2,1,0:T(8,128)(2,1)S(1)}, bf16[4,256,512]{2,1,0:T(8,128)(2,1)}, u32[]{:S(2)}) copy-start(bf16[4,256,512]{2,1,0:T(8,128)(2,1)} %get-tuple-element.202) | copy-start | bytes 3145732
  232.9 3.2 %copy-start.3 = (f32[1024,512]{1,0:T(8,128)S(1)}, f32[1024,512]{1,0:T(8,128)}, u32[]{:S(2)}) copy-start(f32[1024,512]{1,0:T(8,128)} %copy-done.2) | copy-start | bytes 6291460
  240.5 3.6 %copy-start.13 = (bf16[4,256,512]{2,1,0:T(8,128)(2,1)S(1)}, bf16[4,256,512]{2,1,0:T(8,128)(2,1)}, u32[]{:S(2)}) copy-start(bf16[4,256,512]{2,1,0:T(8,128)(2,1)} %get-tuple-element.204) | copy-start | bytes 3145732
  244.1 3.3 %copy-start.6 = (bf16[4,256,512]{2,1,0:T(8,128)(2,1)S(1)}, bf16[4,256,512]{2,1,0:T(8,128)(2,1)}, u32[]{:S(2)}) copy-start(bf16[4,256,512]{2,1,0:T(8,128)(2,1)} %copy-done.5) | copy-start | bytes 3145732
  247.4 4.9 %copy-start.1 = (bf16[18,512]{1,0:T(8,128)(2,1)S(1)}, bf16[18,512]{1,0:T(8,128)(2,1)}, u32[]{:S(2)}) copy-start(bf16[18,512]{1,0:T(8,128)(2,1)} %param.43) | copy-start | bytes 55300
Sparse Core Ops, SparseCore 0:
  19.7 51.3 all-gather.2
